TPU v7x, 32 devices: a whole 2x2x4 slice. The times are simulated.
32 devices in a mesh: head: 2 (over x), inner: 4 (over y, core), outer: 4 (over z).
Axes of the slice: x: 2, y: 2, z: 4, core: 2. Of those that a mesh axis runs over, the one named last changes fastest.
Arguments:
- queries: float32 [2048, 8, 128], P(('inner', 'outer'), 'head'), may hold values from -8 to 8
- key_rows: float32 [2048, 128], P(('inner', 'outer'), 'head'), may hold values from -8 to 8
- values: float32 [2048, 128], P(('inner', 'outer'), 'head'), may hold values from -24 to 24
- out_grad: float32 [2048, 8, 128], P(('inner', 'outer'), 'head'), may hold values from -48 to 48
- sink_len: int32 [1], replicated, may hold values from 32 to 128
- window_len: int32 [1], replicated, may hold values from 129 to 640
- block_codes: int32 [16, 5], replicated, may hold values from 0 to 2, as said below
Outputs:
- query_grad: float32 [2048, 8, 128], P(('inner', 'outer'), 'head')
- key_grad: float32 [2048, 128], P(('inner', 'outer'), 'head')
- value_grad: float32 [2048, 128], P(('inner', 'outer'), 'head')
Inputs may be any that keep to these rules, and one draw needn't show every extreme that they name: block_codes[b, 0] is 1 or 2 for every block b.
All inputs are finite; a program needn't handle non-finite values.
Results may differ from a plain program's by a relative error of at most 0.0003.
Values sent between devices are 32-bit elements; how exact they have to be, the bound alone decides.
A program may use at most 64 MiB of HBM per device.

v0:
```python
import functools
import math

import jax
import jax.numpy as jnp
from jax import lax
from jax.experimental import pallas as pl
from jax.experimental.pallas import tpu as pltpu
from jax.sharding import PartitionSpec as P

STEPS = 5
FAR = STEPS - 1
BIG = 1 << 28
very_low = -1e30
f32, bf16 = jnp.float32, jnp.bfloat16
MESH = pl.DeviceIdType.MESH
NT = (((1,), (1,)), ((), ()))
NN = (((1,), (0,)), ((), ()))


def dot(a, b, dims):
    return lax.dot_general(a, b, dims, preferred_element_type=f32)


def two(x):
    hi = x.astype(bf16)
    return hi, (x - hi.astype(f32)).astype(bf16)


def three(x):
    hi = x.astype(bf16)
    rest = x - hi.astype(f32)
    mid = rest.astype(bf16)
    return hi, mid, (rest - mid.astype(f32)).astype(bf16)


def kernel(
    sizes, sink_ref, window_ref, codes_hbm, q_hbm, k_hbm, v_hbm, g_hbm, dq_ref, dkv_ref,
    codes_ref, q_ref, g_ref, load, buf, sinkb, piece, qcat, gcat, st, dp, dshi, dslo, ktcat,
    xout, xin, mine, gout, gin, g4out, g4in, sg, sin, s2, s2in, s3, s3in, send, recv,
):
    ni, no, heads_dev = sizes
    half, block = k_hbm.shape
    rows = q_ref.shape[0]
    temper = 1.0 / math.sqrt(2 * half)
    head, inner, outer = lax.axis_index("head"), lax.axis_index("inner"), lax.axis_index("outer")
    par = lax.rem(head, 2)
    other = 1 - par
    partner = head + 1 - 2 * par
    count = ni * no
    b = inner * no + outer
    pr = block // ni

    def seq(o):
        t = lax.rem(b + o + count, count)
        return (head, t // no, lax.rem(t, no))

    across = (partner, inner, outer)
    columns = [(p, d) for p in range(2) for d in range(ni) if p or d]

    def column(p, d):
        return (partner if p else head, lax.rem(inner + d, ni), outer)

    def source(d):
        return lax.rem(inner - d + ni, ni)

    slots = {}

    def sem(name):
        return slots.setdefault(name, len(slots))

    pending = []

    def copy(name, src, dst, device):
        k = sem(name)
        return pltpu.make_async_remote_copy(
            src_ref=src, dst_ref=dst, send_sem=send.at[k], recv_sem=recv.at[k],
            device_id=device, device_id_type=MESH,
        )

    def start(name, src, dst, device):
        c = copy(name, src, dst, device)
        c.start()
        pending.append(c)

    def arrived(name, dst):
        copy(name, dst, dst, across).wait_recv()

    moves = [
        (k_hbm, buf.at[0, par, 0:half]), (v_hbm, buf.at[0, par, half:2 * half]),
        (q_hbm, q_ref), (g_hbm, g_ref),
        (codes_hbm, codes_ref),
    ]
    loads = [pltpu.make_async_copy(x, y, load.at[i]) for i, (x, y) in enumerate(moves)]
    for x in loads:
        x.start()

    barrier = pltpu.get_barrier_semaphore()
    greet = [seq(s * o) for o in range(1, STEPS) for s in (1, -1)]
    greet += [column(p, d) for p, d in columns]
    greet += [(head, inner, lax.rem(outer + d, no)) for d in range(1, no)]
    for device in greet:
        pl.semaphore_signal(barrier, inc=1, device_id=device, device_id_type=MESH)

    for x in loads:
        x.wait()
    q0, q1, q2 = three(q_ref[...])
    qcat[...] = jnp.concatenate([q0, q1, q0, q1, q2, q0], 1)
    g0, g1, g2 = three(g_ref[...])
    gcat[...] = jnp.concatenate([g0, g1, g0, g1, g2, g0], 1)
    pl.semaphore_wait(barrier, len(greet))

    own = buf.at[0, par]
    first = (inner == 0) & (outer == 0)
    top = outer == 0
    at_root = piece

    @pl.when(first)
    def _():
        for i in range(1, ni):
            copy(f"f1_{i}", own.at[pl.ds(i * pr, pr)], at_root, (head, i, outer)).start()
        piece[...] = buf[0, par, 0:pr, :]

    start("x0", own, own, across)
    for o in range(FAR, 0, -1):
        start(f"w{o}", own, buf.at[o, par], seq(o))

    def scores_of(a, c, index, allowed):
        keys = jnp.concatenate([a[0:half], c[0:half]], 0)
        vals = jnp.concatenate([a[half:], c[half:]], 0)
        k0, k1, k2 = three(keys.T)
        v0, v1, v2 = three(vals.T)
        s = dot(jnp.concatenate([k0, k0, k1, k1, k0, k2], 1), qcat[...], NT)
        st[index] = jnp.where(allowed, temper * s, very_low)
        dp[index] = dot(jnp.concatenate([v0, v0, v1, v1, v0, v2], 1), gcat[...], NT)
        t0, t1 = two(keys * temper)
        ktcat[index] = jnp.concatenate([t0, t1, t0], 1)

    jk = lax.broadcasted_iota(jnp.int32, (block, rows), 0)
    iq = lax.broadcasted_iota(jnp.int32, (block, rows), 1) // heads_dev
    gap = iq - jk
    sink_end, window = sink_ref[0], window_ref[0]

    def mask_of(o):
        code = codes_ref[o, b]
        limit = jnp.where(code == 2, BIG, jnp.where(code == 1, window, -BIG))
        limit = jnp.where(b >= o, limit, -BIG) - o * block
        here = jnp.where(b == o, sink_end, 0)
        if o == 0:
            return (gap >= 0) & ((gap < limit) | (jk < here))
        return (gap < limit) & (jk >= here)

    def slot(o):
        scores_of(buf[o, 0], buf[o, 1], o, mask_of(o))

    arrived("x0", buf.at[0, other])
    start("w4x", buf.at[0, other], buf.at[FAR, other], seq(FAR))

    @pl.when(top)
    def _():
        @pl.when(inner != 0)
        def _():
            for i in range(1, ni):
                @pl.when(inner == i)
                def _():
                    arrived(f"f1_{i}", piece)
        for z in range(1, no):
            copy(f"f2_{z}", piece, piece, (head, inner, z)).start()

    slot(0)
    def relay(order):
        for o in order:
            arrived(f"w{o}", buf.at[o, par])
            copy(f"r{o}", buf.at[o, par], buf.at[o, par], across).start()

    up = list(range(1, FAR))

    @pl.when(outer == 0)
    def _():
        relay(up[::-1])

    @pl.when(outer == no - 1)
    def _():
        relay(up)

    @pl.when((outer != 0) & (outer != no - 1))
    def _():
        relay(up[::2] + up[1::2])

    for o in up:
        pending.append(copy(f"r{o}", buf.at[o, par], buf.at[o, par], across))

    @pl.when(outer != 0)
    def _():
        for z in range(1, no):
            @pl.when(outer == z)
            def _():
                arrived(f"f2_{z}", piece)

    where = pl.ds(pl.multiple_of(inner * pr, pr), pr)
    for p, d in columns:
        start(f"f3_{p}_{d}", piece, sinkb.at[par, where], column(p, d))
    sinkb[par, where] = piece[...]

    arrived(f"w{FAR}", buf.at[FAR, par])
    arrived("w4x", buf.at[FAR, other])
    slot(FAR)
    for o in range(1, FAR):
        arrived(f"r{o}", buf.at[o, other])
        slot(o)
    for p, d in columns:
        there = pl.ds(pl.multiple_of(source(d) * pr, pr), pr)
        arrived(f"f3_{p}_{d}", sinkb.at[other if p else par, there])
    scores_of(sinkb[0], sinkb[1], STEPS, jk < jnp.where(b >= 1, sink_end, 0))

    total = STEPS + 1
    top_score = jnp.max(st[0], axis=0, keepdims=True)
    for i in range(1, total):
        top_score = jnp.maximum(top_score, jnp.max(st[i], axis=0, keepdims=True))
    norm = jnp.zeros((1, rows), f32)
    delta = jnp.zeros((1, rows), f32)
    for i in range(total):
        e = jnp.exp(st[i] - top_score)
        st[i] = e
        norm = norm + jnp.sum(e, axis=0, keepdims=True)
        delta = delta + jnp.sum(e * dp[i], axis=0, keepdims=True)
    scale = 1.0 / norm
    delta = delta * scale

    def grads(i):
        probs = st[i] * scale
        ds = probs * (dp[i] - delta)
        p_hi, p_lo = two(probs)
        d_hi, d_lo = two(ds)
        dshi[i] = d_hi
        dslo[i] = d_lo
        w = 2 * half
        pv = dot(p_hi, gcat[:, 0:2 * w], NN)
        dv = pv[:, 0:w] + pv[:, w:] + dot(p_lo, gcat[:, 0:w], NN)
        kq = dot(d_hi, qcat[:, 0:2 * w], NN)
        dk = temper * (kq[:, 0:w] + kq[:, w:] + dot(d_lo, qcat[:, 0:w], NN))
        dk, dv = dk.T, dv.T
        even = jnp.concatenate([dk[0:half], dv[0:half]], 0)
        odd = jnp.concatenate([dk[half:], dv[half:]], 0)
        keep = jnp.where(par == 0, even, odd)
        give = jnp.where(par == 0, odd, even)
        return keep, give

    def pass_on(o):
        arrived(f"gx{o}", xin.at[o])
        gout[o] = mine[o] + xin[o]
        start(f"gz{o}", gout.at[o], gin.at[o], seq(-o))

    def near(o):
        keep, give = grads(o)
        mine[o] = keep
        xout[o] = give
        start(f"gx{o}", xout.at[o], xin.at[o], across)

    keep, give = grads(STEPS)
    sg[0] = keep
    sg[1] = give
    for p, d in columns:
        target = lax.rem(inner + d, ni)
        rng = pl.ds(pl.multiple_of(target * pr, pr), pr)
        start(f"b1_{p}_{d}", sg.at[p, rng], sin.at[p * ni + d], column(p, d))

    near(FAR - 1)
    near(FAR - 2)
    pass_on(FAR - 1)
    keep, give = grads(FAR)
    g4out[0] = keep
    g4out[1] = give
    start("g4k", g4out.at[0], g4in.at[0], seq(-FAR))
    start("g4g", g4out.at[1], g4in.at[1], seq(-FAR))

    for o in range(FAR - 3, 0, -1):
        near(o)
        pass_on(o + 1)
    for p, d in columns:
        arrived(f"b1_{p}_{d}", sin.at[p * ni + d])
    acc = sg[0, where]
    for p, d in columns:
        acc = acc + sin[p * ni + d]
    s2[...] = acc
    for z in range(1, no):
        @pl.when(outer == z)
        def _():
            copy(f"b2_{z}", s2, s2in.at[z], (head, inner, 0)).start()

    keep, give = grads(0)
    arrived("g4g", g4in.at[1])
    xout[0] = give + g4in[1]
    start("gx0", xout.at[0], xin.at[0], across)
    pass_on(1)
    arrived("g4k", g4in.at[0])
    mine[0] = keep + g4in[0]

    dqt = jnp.zeros((2 * half, rows), f32)
    for i in range(total):
        hi = dshi[i]
        dqt = dqt + dot(ktcat[i], jnp.concatenate([hi, hi, dslo[i]], 0), NN)
    dq_ref[...] = dqt.T

    @pl.when(top)
    def _():
        part = s2[...]
        for z in range(1, no):
            arrived(f"b2_{z}", s2in.at[z])
            part = part + s2in[z]
        s3[...] = part
        for i in range(1, ni):
            @pl.when(inner == i)
            def _():
                copy(f"b3_{i}", s3, s3in.at[i], (head, 0, outer)).start()

    arrived("gx0", xin.at[0])
    acc = mine[0] + xin[0]
    for o in range(FAR - 1, 0, -1):
        arrived(f"gz{o}", gin.at[o])
        acc = acc + gin[o]
    mine[0] = acc

    @pl.when(first)
    def _():
        mine[0, 0:pr] += s3[...]
        for i in range(1, ni):
            arrived(f"b3_{i}", s3in.at[i])
            mine[0, i * pr:(i + 1) * pr] += s3in[i]

    dkv_ref[...] = mine[0]

    for c in pending:
        c.wait_send()

    @pl.when(first)
    def _():
        for i in range(1, ni):
            copy(f"f1_{i}", own.at[pl.ds(i * pr, pr)], at_root, (head, i, outer)).wait_send()

    @pl.when(top)
    def _():
        for z in range(1, no):
            copy(f"f2_{z}", piece, piece, (head, inner, z)).wait_send()
        for i in range(1, ni):
            @pl.when(inner == i)
            def _():
                copy(f"b3_{i}", s3, s3in.at[i], (head, 0, outer)).wait_send()

    for z in range(1, no):
        @pl.when(outer == z)
        def _():
            copy(f"b2_{z}", s2, s2in.at[z], (head, inner, 0)).wait_send()
    assert len(slots) <= send.shape[0]


def store(dq_ref, dkv_ref, dq_hbm, dk_hbm, dv_hbm, sem):
    half = dk_hbm.shape[0]
    moves = [
        (dq_ref, dq_hbm), (dkv_ref.at[0:half], dk_hbm), (dkv_ref.at[half:2 * half], dv_hbm),
    ]
    copies = [pltpu.make_async_copy(x, y, sem.at[i]) for i, (x, y) in enumerate(moves)]
    for c in copies:
        c.start()
    for c in copies:
        c.wait()


def shards(ni, no, queries, key_rows, values, out_grad, sink_len, window_len, block_codes):
    block, heads_dev, dim = queries.shape
    rows = block * heads_dev
    half = key_rows.shape[1]
    codes = block_codes.T
    pr = block // ni
    total = STEPS + 1
    sems = 2 * (ni - 1) + 2 * (no - 1) + 2 * (2 * ni - 1) + 4 * STEPS
    smem = pl.BlockSpec(memory_space=pltpu.SMEM)
    vmem, hbm = pl.BlockSpec(memory_space=pltpu.VMEM), pl.BlockSpec(memory_space=pltpu.HBM)
    tile = (block, dim)
    grad_q, grad_kv = pl.pallas_call(
        functools.partial(kernel, (ni, no, heads_dev)),
        out_shape=(
            pltpu.VMEM((rows, dim), f32),
            pltpu.VMEM((2 * half, block), f32),
        ),
        in_specs=[smem] * 2 + [hbm] * 5,
        out_specs=(vmem,) * 2,
        scratch_shapes=[
            pltpu.SMEM(codes.shape, jnp.int32),
            pltpu.VMEM((rows, dim), f32),
            pltpu.VMEM((rows, dim), f32),
            pltpu.SemaphoreType.DMA((5,)),
            pltpu.VMEM((STEPS, 2) + tile, f32),
            pltpu.VMEM((2,) + tile, f32),
            pltpu.VMEM((pr, dim), f32),
            pltpu.VMEM((rows, 6 * dim), bf16),
            pltpu.VMEM((rows, 6 * dim), bf16),
            pltpu.VMEM((total, block, rows), f32),
            pltpu.VMEM((total, block, rows), f32),
            pltpu.VMEM((total, block, rows), bf16),
            pltpu.VMEM((total, block, rows), bf16),
            pltpu.VMEM((total, dim, 3 * block), bf16),
            pltpu.VMEM((FAR,) + tile, f32),
            pltpu.VMEM((FAR,) + tile, f32),
            pltpu.VMEM((FAR,) + tile, f32),
            pltpu.VMEM((FAR,) + tile, f32),
            pltpu.VMEM((FAR,) + tile, f32),
            pltpu.VMEM((2,) + tile, f32),
            pltpu.VMEM((2,) + tile, f32),
            pltpu.VMEM((2,) + tile, f32),
            pltpu.VMEM((2 * ni, pr, dim), f32),
            pltpu.VMEM((pr, dim), f32),
            pltpu.VMEM((no, pr, dim), f32),
            pltpu.VMEM((pr, dim), f32),
            pltpu.VMEM((ni, pr, dim), f32),
            pltpu.SemaphoreType.DMA((sems,)),
            pltpu.SemaphoreType.DMA((sems,)),
        ],
        compiler_params=pltpu.CompilerParams(
            collective_id=0, has_side_effects=True, vmem_limit_bytes=66_000_000
        ),
    )(
        sink_len, window_len, codes,
        queries.reshape(rows, dim), key_rows.T, values.T, out_grad.reshape(rows, dim),
    )
    grad_q, grad_k, grad_v = pl.pallas_call(
        store,
        out_shape=(
            jax.ShapeDtypeStruct((rows, dim), f32),
            jax.ShapeDtypeStruct((half, block), f32),
            jax.ShapeDtypeStruct((half, block), f32),
        ),
        in_specs=[vmem] * 2,
        out_specs=(hbm,) * 3,
        scratch_shapes=[pltpu.SemaphoreType.DMA((3,))],
        compiler_params=pltpu.CompilerParams(vmem_limit_bytes=1 << 20),
    )(grad_q, grad_kv)
    return grad_q.reshape(queries.shape), grad_k.T, grad_v.T


def solution(mesh):
    in_specs = (
        P(("inner", "outer"), "head", None),
        P(("inner", "outer"), "head"),
        P(("inner", "outer"), "head"),
        P(("inner", "outer"), "head", None),
        P(),
        P(),
        P(),
    )
    out_specs = (
        P(("inner", "outer"), "head", None),
        P(("inner", "outer"), "head"),
        P(("inner", "outer"), "head"),
    )
    body = functools.partial(shards, mesh.shape["inner"], mesh.shape["outer"])
    return jax.shard_map(body, mesh=mesh, in_specs=in_specs, out_specs=out_specs, check_vma=False)
```

profile of v0, /device:TPU:0, one launch (start us, length us, event | category | flops | bytes accessed | tf_op | source)
XLA Modules:
  0.0 38.4 jit_solution(14687665857220855693)
XLA Ops:
  1.9 35.8 %shard_map.94 = (f32[512,128]{1,0:T(8,128)S(1)}, f32[128,128]{1,0:T(8,128)S(1)}) custom-call(s32[1]{0:T(128)S(6)} %copy.10.sink_ref, s32[1]{0:T(128)S(6)} %copy.11.window_ref, s32[5,16]{1,0:T(8,128)} %bitcast.12, f32[512,128]{1,0:T(8,128)} %bitcast.8, f32[64,128]{1,0:T(8,128)} %bitcast.10, f32[64,128]{1,0:T(8,128)} %bitcast.11, f32[512,128]{1,0:T(8,128)} %bitcast.9), custom_call_target="tpu_custom_call" | custom-call | tf_op jit(solution)/shard_map/pallas_call | solution.py:380
  37.7 0.7 %shard_map.95 = (f32[512,128]{1,0:T(8,128)}, f32[64,128]{1,0:T(8,128)}, f32[64,128]{1,0:T(8,128)}) custom-call(f32[512,128]{1,0:T(8,128)S(1)} %get-tuple-element.8.dq_ref, f32[128,128]{1,0:T(8,128)S(1)} %get-tuple-element.9.dkv_ref), custom_call_target="tpu_custom_call" | custom-call | tf_op jit(solution)/shard_map/pallas_call | solution.py:426
where the time goes:
time: 38.6 us; the launch traced here: 38.4 us
  Pallas kernels  36.5 us (95%)
  between operations  1.93 us (5%)
    pallas_call x1, Pallas kernels, shards(): pl.pallas_call(functools.partial(kernel, (ni, no, heads_dev)), out_shape=...  35.8 us

commit v1 on v0

v1 whole, which is shorter than its diff:
```python
import functools
import math

import jax
import jax.numpy as jnp
from jax import lax
from jax.experimental import pallas as pl
from jax.experimental.pallas import tpu as pltpu
from jax.sharding import PartitionSpec as P

STEPS = 5
FAR = STEPS - 1
BIG = 1 << 28
very_low = -1e30
f32, bf16 = jnp.float32, jnp.bfloat16
MESH = pl.DeviceIdType.MESH
NT = (((1,), (1,)), ((), ()))
NN = (((1,), (0,)), ((), ()))


def dot(a, b, dims):
    return lax.dot_general(a, b, dims, preferred_element_type=f32)


def two(x):
    hi = x.astype(bf16)
    return hi, (x - hi.astype(f32)).astype(bf16)


def when(cond, f):
    if cond is None:
        f()
    else:
        pl.when(cond)(f)


def kernel(
    sizes, sink_hbm, window_hbm, codes_hbm, q_hbm, k_hbm, v_hbm, g_hbm, dq_ref, dkv_ref,
    sink_ref, window_ref, codes_ref, q_ref, g_ref, load, buf, sinkb, piece, qcat, gcat,
    st, dp, peak, run, ds, ktcat, xout, xin, mine, gout, gin, g4out, g4in, sg, sin, s2, s2in,
    dqt, send, recv,
):
    ni, no, heads_dev = sizes
    half, block = k_hbm.shape
    rows = q_ref.shape[0]
    temper = 1.0 / math.sqrt(2 * half)
    head, inner, outer = lax.axis_index("head"), lax.axis_index("inner"), lax.axis_index("outer")
    par = lax.rem(head, 2)
    other = 1 - par
    partner = head + 1 - 2 * par
    count = ni * no
    b = inner * no + outer
    pr = block // ni

    def seq(o):
        t = lax.rem(b + o + count, count)
        return (head, t // no, lax.rem(t, no))

    across = (partner, inner, outer)
    columns = [(p, d) for p in range(2) for d in range(ni) if p or d]
    first = (inner == 0) & (outer == 0)
    top = outer == 0

    def column(p, d):
        return (partner if p else head, lax.rem(inner + d, ni), outer)

    def up(o):
        return b + o < count

    def down(o):
        return b >= o

    slots = {}

    def sem(name):
        return slots.setdefault(name, len(slots))

    pending = []

    def copy(name, src, dst, device):
        return pltpu.make_async_remote_copy(
            src_ref=src, dst_ref=dst, send_sem=send.at[sem(name)], recv_sem=recv.at[sem(name)],
            device_id=device, device_id_type=MESH,
        )

    def start(name, src, dst, device, cond=None, sent=True):
        c = copy(name, src, dst, device)
        when(cond, c.start)
        if sent:
            pending.append((cond, c))

    def sent(name, like, cond=None):
        pending.append((cond, copy(name, like, like, across)))

    def arrived(name, dst):
        copy(name, dst, dst, across).wait_recv()

    moves = [
        (k_hbm, buf.at[0, par, 0:half]), (v_hbm, buf.at[0, par, half:2 * half]),
        (q_hbm, q_ref), (g_hbm, g_ref),
        (codes_hbm, codes_ref), (sink_hbm, sink_ref), (window_hbm, window_ref),
    ]
    loads = [pltpu.make_async_copy(x, y, load.at[i]) for i, (x, y) in enumerate(moves)]

    barrier = pltpu.get_barrier_semaphore()

    def greet(device):
        pl.semaphore_signal(barrier, inc=1, device_id=device, device_id_type=MESH)

    for p, d in columns:
        greet(column(p, d))
    expect = len(columns)
    for o in range(1, STEPS):
        when(up(o), lambda: greet(seq(o)))
        when(down(o), lambda: greet(seq(-o)))
        expect = expect + up(o).astype(jnp.int32) + down(o).astype(jnp.int32)
    when(outer != 0, lambda: greet((head, inner, 0)))
    expect = expect + jnp.where(top, no - 1, 0) + jnp.where(first, 0, 1)

    @pl.when(first)
    def _():
        for i in range(ni):
            for z in range(no):
                if i or z:
                    greet((head, i, z))

    for x in loads:
        x.start()
    pl.semaphore_wait(barrier, expect)

    def own_to(name, o, dst, device, cond=None):
        start(name, k_hbm, dst.at[0:half], device, cond, False)
        start(name, v_hbm, dst.at[half:2 * half], device, cond, False)
        sent(name, dst, cond)

    def rows_of(i):
        return (k_hbm.at[pl.ds(i * pr, pr)] if i * pr < half
                else v_hbm.at[pl.ds(i * pr - half, pr)])

    for i in range(ni):
        for p in range(2):
            if i or p:
                to = (partner if p else head, i, 0)
                start(f"f1_{p}", rows_of(i), piece.at[par], to, first, False)
    sent("f1_0", buf.at[0, 0, 0:(ni - 1) * pr], first)
    sent("f1_1", buf.at[0, 0], first)

    own_to("x0", 0, buf.at[0, par], across)
    for o in (3, 2, 1, 4):
        own_to(f"w{o}", o, buf.at[o, par], seq(o), up(o))

    loads[2].wait()
    q0, q1 = two(q_ref[...])
    qcat[...] = jnp.concatenate([q0, q1], 1)
    loads[3].wait()
    g0, g1 = two(g_ref[...])
    gcat[...] = jnp.concatenate([g0, g1], 1)
    for i in (0, 1, 4, 5, 6):
        loads[i].wait()

    @pl.when(first)
    def _():
        piece[par] = buf[0, par, 0:pr, :]

    jk = lax.broadcasted_iota(jnp.int32, (block, rows), 0)
    iq = lax.broadcasted_iota(jnp.int32, (block, rows), 1) // heads_dev
    gap = iq - jk
    sink_end, window = sink_ref[0], window_ref[0]

    def mask_of(o):
        code = codes_ref[o, b]
        limit = jnp.where(code == 2, BIG, jnp.where(code == 1, window, -BIG)) - o * block
        here = jnp.where(b == o, sink_end, 0)
        if o == 0:
            return (gap >= 0) & ((gap < limit) | (jk < here))
        return (gap < limit) & (jk >= here)

    def scores_of(keys, vals, index, allowed):
        k0, k1 = two(keys.T)
        v0, v1 = two(vals.T)
        kk = jnp.concatenate([jnp.concatenate([k0, k0], 1), jnp.concatenate([k1, k1], 1)], 0)
        vv = jnp.concatenate([jnp.concatenate([v0, v0], 1), jnp.concatenate([v1, v1], 1)], 0)
        s = dot(kk, qcat[...], NT)
        s = jnp.where(allowed, temper * (s[0:block] + s[block:]), very_low)
        d = dot(vv, gcat[...], NT)
        d = d[0:block] + d[block:]
        t0, t1 = two(keys * temper)
        ktcat[index] = jnp.concatenate([t0, t1, t0], 1)
        high = jnp.max(s, axis=0, keepdims=True)
        if index:
            before = run[0:1]
            high = jnp.maximum(high, before)
            shrink = jnp.exp(before - high)
        e = jnp.exp(s - high)
        st[index] = e
        dp[index] = d
        norm = jnp.sum(e, axis=0, keepdims=True)
        delta = jnp.sum(e * d, axis=0, keepdims=True)
        if index:
            norm = norm + shrink * run[1:2]
            delta = delta + shrink * run[2:3]
        peak[index:index + 1] = high
        run[0:1] = high
        run[1:2] = norm
        run[2:3] = delta

    def slot(o):
        def _():
            a, c = buf[o, 0], buf[o, 1]
            scores_of(
                jnp.concatenate([a[0:half], c[0:half]], 0),
                jnp.concatenate([a[half:], c[half:]], 0), o, mask_of(o),
            )
        return _

    @pl.when(top)
    def _():
        @pl.when(jnp.logical_not(first))
        def _():
            arrived("f1_0", piece.at[par])
        arrived("f1_1", piece.at[other])
    for z in range(1, no):
        start("f2", piece, piece, (head, inner, z), top, False)
    sent("f2", sinkb.at[0:no - 1], top)

    arrived("x0", buf.at[0, other])
    start("w4x", buf.at[0, other], buf.at[FAR, other], seq(FAR), up(FAR))
    slot(0)()

    def relay(o):
        def _():
            arrived(f"w{o}", buf.at[o, par])
            copy(f"r{o}", buf.at[o, par], buf.at[o, par], across).start()
        when(down(o), _)

    def relays(order):
        def _():
            for o in order:
                relay(o)
        return _

    near = list(range(1, FAR))
    when(outer == 0, relays(near[::-1]))
    when(outer == no - 1, relays(near))
    when((outer != 0) & (outer != no - 1), relays(near[::2] + near[1::2]))
    for o in near:
        pending.append((down(o), copy(f"r{o}", buf.at[o, par], buf.at[o, par], across)))

    @pl.when(outer != 0)
    def _():
        arrived("f2", piece)
    for d in range(1, ni):
        start("f3", piece, sinkb.at[inner], column(0, d), None, False)
    sent("f3", sinkb.at[0:ni - 1])
    sinkb[inner] = piece[...]

    @pl.when(down(FAR))
    def _():
        arrived(f"w{FAR}", buf.at[FAR, par])
        arrived("w4x", buf.at[FAR, other])
        slot(FAR)()

    for o in near:
        @pl.when(down(o))
        def _():
            arrived(f"r{o}", buf.at[o, other])
            slot(o)()

    arrived("f3", sinkb.at[0:ni - 1])

    @pl.when(b >= 1)
    def _():
        a = [sinkb[i, p] for p in range(2) for i in range(ni)]
        cut = ni // 2
        keys = jnp.concatenate(a[0:cut] + a[ni:ni + cut], 0)
        vals = jnp.concatenate(a[cut:ni] + a[ni + cut:], 0)
        scores_of(keys, vals, STEPS, jk < sink_end)

    high = run[0:1]
    scale = 1.0 / run[1:2]
    delta = run[2:3] * scale

    def grads(i):
        probs = st[i] * (jnp.exp(peak[i:i + 1] - high) * scale)
        score = probs * (dp[i] - delta)
        p_hi, p_lo = two(probs)
        d_hi, d_lo = two(score)
        ds[i, 0] = d_hi
        ds[i, 1] = d_lo
        w = 2 * half
        pv = dot(jnp.concatenate([p_hi, p_lo], 0), gcat[...], NN)
        dv = pv[0:block, 0:w] + pv[0:block, w:] + pv[block:, 0:w]
        kq = dot(jnp.concatenate([d_hi, d_lo], 0), qcat[...], NN)
        dk = temper * (kq[0:block, 0:w] + kq[0:block, w:] + kq[block:, 0:w])
        dk, dv = dk.T, dv.T
        even = jnp.concatenate([dk[0:half], dv[0:half]], 0)
        odd = jnp.concatenate([dk[half:], dv[half:]], 0)
        keep = jnp.where(par == 0, even, odd)
        give = jnp.where(par == 0, odd, even)
        return keep, give

    @pl.when(b >= 1)
    def _():
        keep, give = grads(STEPS)
        sg[0] = keep
        sg[1] = give

    @pl.when(b == 0)
    def _():
        sg[...] = jnp.zeros_like(sg)

    for p, d in columns:
        target = lax.rem(inner + d, ni)
        rng = pl.ds(pl.multiple_of(target * pr, pr), pr)
        start("b1", sg.at[p, rng], sin.at[p * ni + d], column(p, d), None, False)
    sent("b1", sin.at[1:2 * ni])

    def give_near(o):
        @pl.when(down(o))
        def _():
            keep, give = grads(o)
            mine[o] = keep
            xout[o] = give
        start(f"gx{o}", xout.at[o], xin.at[o], across, down(o))

    def pass_on(o):
        @pl.when(down(o))
        def _():
            arrived(f"gx{o}", xin.at[o])
            gout[o] = mine[o] + xin[o]
        start(f"gz{o}", gout.at[o], gin.at[o], seq(-o), down(o))

    give_near(3)
    give_near(2)

    @pl.when(down(FAR))
    def _():
        keep, give = grads(FAR)
        g4out[0] = keep
        g4out[1] = give
    start("g4", g4out, g4in, seq(-FAR), down(FAR))
    give_near(1)

    where = pl.ds(pl.multiple_of(inner * pr, pr), pr)
    arrived("b1", sin.at[1:2 * ni])
    acc = sg[0, where]
    for p, d in columns:
        acc = acc + sin[p * ni + d]
    s2[...] = acc
    for i in range(ni):
        for z in range(no):
            if i or z:
                mine_here = (inner == i) & (outer == z)
                start("b2", s2, s2in.at[i * no + z], (head, 0, 0), mine_here, False)
    sent("b2", s2, jnp.logical_not(first))

    pass_on(3)
    keep, give = grads(0)
    mine[0] = keep
    xout[0] = give
    pass_on(2)

    @pl.when(up(FAR))
    def _():
        arrived("g4", g4in)
        mine[0] += g4in[0]
        xout[0] += g4in[1]
    start("gx0", xout.at[0], xin.at[0], across)
    pass_on(1)

    def dq_part(i):
        hi = ds[i, 0]
        return dot(ktcat[i], jnp.concatenate([hi, hi, ds[i, 1]], 0), NN)

    dqt[...] = dq_part(0)
    for i in range(1, STEPS + 1):
        @pl.when(b >= (i if i < STEPS else 1))
        def _():
            dqt[...] += dq_part(i)
    dq_ref[...] = dqt[...].T

    arrived("gx0", xin.at[0])
    dkv_ref[...] = mine[0] + xin[0]
    for o in range(FAR - 1, 0, -1):
        @pl.when(up(o))
        def _():
            arrived(f"gz{o}", gin.at[o])
            dkv_ref[...] += gin[o]

    @pl.when(first)
    def _():
        arrived("b2", s2in.at[1:ni * no])
        for i in range(ni):
            part = s2in[i * no] if i else s2[...]
            for z in range(1, no):
                part = part + s2in[i * no + z]
            dkv_ref[i * pr:(i + 1) * pr] += part

    for cond, c in pending:
        when(cond, c.wait_send)
    assert len(slots) <= send.shape[0], len(slots)


def store(dq_ref, dkv_ref, dq_hbm, dk_hbm, dv_hbm, sem):
    half = dk_hbm.shape[0]
    moves = [
        (dq_ref, dq_hbm), (dkv_ref.at[0:half], dk_hbm), (dkv_ref.at[half:2 * half], dv_hbm),
    ]
    copies = [pltpu.make_async_copy(x, y, sem.at[i]) for i, (x, y) in enumerate(moves)]
    for c in copies:
        c.start()
    for c in copies:
        c.wait()


def shards(ni, no, queries, key_rows, values, out_grad, sink_len, window_len, block_codes):
    block, heads_dev, dim = queries.shape
    rows = block * heads_dev
    half = key_rows.shape[1]
    codes = block_codes.T
    pr = block // ni
    total = STEPS + 1
    sems = 23
    vmem, hbm = pl.BlockSpec(memory_space=pltpu.VMEM), pl.BlockSpec(memory_space=pltpu.HBM)
    tile = (block, dim)
    grad_q, grad_kv = pl.pallas_call(
        functools.partial(kernel, (ni, no, heads_dev)),
        out_shape=(
            pltpu.VMEM((rows, dim), f32),
            pltpu.VMEM((2 * half, block), f32),
        ),
        in_specs=[hbm] * 7,
        out_specs=(vmem,) * 2,
        scratch_shapes=[
            pltpu.SMEM(sink_len.shape, jnp.int32),
            pltpu.SMEM(window_len.shape, jnp.int32),
            pltpu.SMEM(codes.shape, jnp.int32),
            pltpu.VMEM((rows, dim), f32),
            pltpu.VMEM((rows, dim), f32),
            pltpu.SemaphoreType.DMA((7,)),
            pltpu.VMEM((STEPS, 2) + tile, f32),
            pltpu.VMEM((ni, 2, pr, dim), f32),
            pltpu.VMEM((2, pr, dim), f32),
            pltpu.VMEM((rows, 2 * dim), bf16),
            pltpu.VMEM((rows, 2 * dim), bf16),
            pltpu.VMEM((total, block, rows), f32),
            pltpu.VMEM((total, block, rows), f32),
            pltpu.VMEM((8, rows), f32),
            pltpu.VMEM((8, rows), f32),
            pltpu.VMEM((total, 2, block, rows), bf16),
            pltpu.VMEM((total, dim, 3 * block), bf16),
            pltpu.VMEM((FAR,) + tile, f32),
            pltpu.VMEM((FAR,) + tile, f32),
            pltpu.VMEM((FAR,) + tile, f32),
            pltpu.VMEM((FAR,) + tile, f32),
            pltpu.VMEM((FAR,) + tile, f32),
            pltpu.VMEM((2,) + tile, f32),
            pltpu.VMEM((2,) + tile, f32),
            pltpu.VMEM((2,) + tile, f32),
            pltpu.VMEM((2 * ni, pr, dim), f32),
            pltpu.VMEM((pr, dim), f32),
            pltpu.VMEM((ni * no, pr, dim), f32),
            pltpu.VMEM((dim, rows), f32),
            pltpu.SemaphoreType.DMA((sems,)),
            pltpu.SemaphoreType.DMA((sems,)),
        ],
        compiler_params=pltpu.CompilerParams(
            collective_id=0, has_side_effects=True, vmem_limit_bytes=66_000_000
        ),
    )(
        sink_len, window_len, codes,
        queries.reshape(rows, dim), key_rows.T, values.T, out_grad.reshape(rows, dim),
    )
    grad_q, grad_k, grad_v = pl.pallas_call(
        store,
        out_shape=(
            jax.ShapeDtypeStruct((rows, dim), f32),
            jax.ShapeDtypeStruct((half, block), f32),
            jax.ShapeDtypeStruct((half, block), f32),
        ),
        in_specs=[vmem] * 2,
        out_specs=(hbm,) * 3,
        scratch_shapes=[pltpu.SemaphoreType.DMA((3,))],
        compiler_params=pltpu.CompilerParams(vmem_limit_bytes=1 << 20),
    )(grad_q, grad_kv)
    return grad_q.reshape(queries.shape), grad_k.T, grad_v.T


def solution(mesh):
    in_specs = (
        P(("inner", "outer"), "head", None),
        P(("inner", "outer"), "head"),
        P(("inner", "outer"), "head"),
        P(("inner", "outer"), "head", None),
        P(),
        P(),
        P(),
    )
    out_specs = (
        P(("inner", "outer"), "head", None),
        P(("inner", "outer"), "head"),
        P(("inner", "outer"), "head"),
    )
    body = functools.partial(shards, mesh.shape["inner"], mesh.shape["outer"])
    return jax.shard_map(body, mesh=mesh, in_specs=in_specs, out_specs=out_specs, check_vma=False)
```

time: 38.6 us -> 34.7 us (0.90)
  Pallas kernels: 36.5 us -> 32.6 us
    pallas_call x1, Pallas kernels: 35.8 us -> 31.9 us  [shards(): pl.pallas_call(functools.partial(kernel, (ni, no, heads_dev)), out_shape=...]
where the time goes in v1:
time: 34.7 us; the launch traced here: 34.5 us
  Pallas kernels  32.6 us (94%)
  between operations  1.93 us (6%)
    pallas_call x1, Pallas kernels, shards(): pl.pallas_call(functools.partial(kernel, (ni, no, heads_dev)), out_shape=...  31.9 us
    pallas_call x1, Pallas kernels, shards(): pl.pallas_call(store, out_shape=(jax.ShapeDtypeStruct((rows, dim), f32),...  0.74 us

profile of v1, /device:TPU:0, one launch (start us, length us, event | category | flops | bytes accessed | tf_op | source)
XLA Modules:
  0.0 34.5 jit_solution(18286370850826144146)
XLA Ops:
  1.9 31.9 %shard_map.94 = (f32[512,128]{1,0:T(8,128)S(1)}, f32[128,128]{1,0:T(8,128)S(1)}) custom-call(s32[1]{0:T(128)S(6)} %copy.10.sink_hbm, s32[1]{0:T(128)S(6)} %copy.11.window_hbm, s32[5,16]{1,0:T(8,128)} %bitcast.12, f32[512,128]{1,0:T(8,128)} %bitcast.8, f32[64,128]{1,0:T(8,128)} %bitcast.10, f32[64,128]{1,0:T(8,128)} %bitcast.11, f32[512,128]{1,0:T(8,128)} %bitcast.9), custom_call_target="tpu_custom_call" | custom-call | tf_op jit(solution)/shard_map/pallas_call | solution.py:426
  33.8 0.7 %shard_map.95 = (f32[512,128]{1,0:T(8,128)}, f32[64,128]{1,0:T(8,128)}, f32[64,128]{1,0:T(8,128)}) custom-call(f32[512,128]{1,0:T(8,128)S(1)} %get-tuple-element.8.dq_ref, f32[128,128]{1,0:T(8,128)S(1)} %get-tuple-element.9.dkv_ref), custom_call_target="tpu_custom_call" | custom-call | tf_op jit(solution)/shard_map/pallas_call | solution.py:474

commit v2 on v1

--- a/solution.py
+++ b/solution.py
@@ -10,6 +10,8 @@
 
 STEPS = 5
 FAR = STEPS - 1
+DIRECT = FAR - 1
+LATE = (2, 3)
 BIG = 1 << 28
 very_low = -1e30
 f32, bf16 = jnp.float32, jnp.bfloat16
@@ -38,7 +40,7 @@
     sizes, sink_hbm, window_hbm, codes_hbm, q_hbm, k_hbm, v_hbm, g_hbm, dq_ref, dkv_ref,
     sink_ref, window_ref, codes_ref, q_ref, g_ref, load, buf, sinkb, piece, qcat, gcat,
     st, dp, peak, run, ds, ktcat, xout, xin, mine, gout, gin, g4out, g4in, sg, sin, s2, s2in,
-    dqt, send, recv,
+    dqt, g3out, g3in, send, recv, late,
 ):
     ni, no, heads_dev = sizes
     half, block = k_hbm.shape
@@ -104,34 +106,64 @@
 
     barrier = pltpu.get_barrier_semaphore()
 
-    def greet(device):
-        pl.semaphore_signal(barrier, inc=1, device_id=device, device_id_type=MESH)
-
-    for p, d in columns:
-        greet(column(p, d))
-    expect = len(columns)
+    def signal(where, device):
+        pl.semaphore_signal(where, inc=1, device_id=device, device_id_type=MESH)
+
+    def late_up(o):
+        return outer + o < no
+
+    def late_down(o):
+        return outer >= o
+
+    def one(cond, n=1):
+        return jnp.where(cond, n, 0)
+
+    def both(o):
+        head_o, inner_o, outer_o = seq(o)
+        return [(head, inner_o, outer_o), (partner, inner_o, outer_o)]
+
+    signal(barrier, across)
+    for d in range(1, ni):
+        signal(barrier, column(0, d))
+    when(top & (inner != 0), lambda: signal(barrier, (partner, 0, 0)))
+    expect = ni + one(first, ni - 1)
     for o in range(1, STEPS):
-        when(up(o), lambda: greet(seq(o)))
-        when(down(o), lambda: greet(seq(-o)))
-        expect = expect + up(o).astype(jnp.int32) + down(o).astype(jnp.int32)
-    when(outer != 0, lambda: greet((head, inner, 0)))
-    expect = expect + jnp.where(top, no - 1, 0) + jnp.where(first, 0, 1)
-
-    @pl.when(first)
-    def _():
-        for i in range(ni):
-            for z in range(no):
-                if i or z:
-                    greet((head, i, z))
+        early = down(o)
+        soon = up(o)
+        if o in LATE:
+            early = early & jnp.logical_not(late_down(o))
+            soon = soon & jnp.logical_not(late_up(o))
+
+            @pl.when(late_up(o))
+            def _():
+                for device in both(o)[:1 + (o == DIRECT)]:
+                    signal(barrier, device)
+            expect = expect + one(late_down(o), 1 + (o == DIRECT))
+
+        @pl.when(early)
+        def _():
+            for device in both(-o)[:1 + (o == DIRECT)]:
+                signal(barrier, device)
+        expect = expect + one(soon, 1 + (o == DIRECT))
 
     for x in loads:
         x.start()
     pl.semaphore_wait(barrier, expect)
-
-    def own_to(name, o, dst, device, cond=None):
-        start(name, k_hbm, dst.at[0:half], device, cond, False)
-        start(name, v_hbm, dst.at[half:2 * half], device, cond, False)
-        sent(name, dst, cond)
+    for o in LATE:
+        @pl.when(late_down(o))
+        def _():
+            for device in both(-o)[:1 + (o == DIRECT)]:
+                signal(late.at[o], device)
+
+    def entered(o):
+        @pl.when(late_up(o))
+        def _():
+            pl.semaphore_wait(late.at[o], 1 + (o == DIRECT))
+
+    def own_to(name, dst, devices, cond=None):
+        for device in devices:
+            start(name, k_hbm, dst.at[0:half], device, cond, False)
+            start(name, v_hbm, dst.at[half:2 * half], device, cond, False)
 
     def rows_of(i):
         return (k_hbm.at[pl.ds(i * pr, pr)] if i * pr < half
@@ -145,9 +177,11 @@
     sent("f1_0", buf.at[0, 0, 0:(ni - 1) * pr], first)
     sent("f1_1", buf.at[0, 0], first)
 
-    own_to("x0", 0, buf.at[0, par], across)
-    for o in (3, 2, 1, 4):
-        own_to(f"w{o}", o, buf.at[o, par], seq(o), up(o))
+    own_to("x0", buf.at[0, par], [across])
+    sent("x0", buf.at[0, 0])
+    for o in (1, FAR):
+        own_to(f"w{o}", buf.at[o, par], [seq(o)], up(o))
+        sent(f"w{o}", buf.at[0, 0], up(o))
 
     loads[2].wait()
     q0, q1 = two(q_ref[...])
@@ -213,46 +247,55 @@
             )
         return _
 
+    entered(2)
+    own_to("w2", buf.at[2, par], [seq(2)], up(2))
+    sent("w2", buf.at[0, 0], up(2))
+
     @pl.when(top)
     def _():
         @pl.when(jnp.logical_not(first))
         def _():
             arrived("f1_0", piece.at[par])
         arrived("f1_1", piece.at[other])
-    for z in range(1, no):
+    start("f2", piece, piece, (head, inner, 1), top, False)
+    entered(DIRECT)
+    for z in range(2, no):
         start("f2", piece, piece, (head, inner, z), top, False)
     sent("f2", sinkb.at[0:no - 1], top)
+    own_to(f"w{DIRECT}", buf.at[DIRECT, par], both(DIRECT), up(DIRECT))
+    sent(f"w{DIRECT}", buf.at[0], up(DIRECT))
 
     arrived("x0", buf.at[0, other])
     start("w4x", buf.at[0, other], buf.at[FAR, other], seq(FAR), up(FAR))
-    slot(0)()
+
+    def spread():
+        for d in range(1, ni):
+            start("f3", piece, sinkb.at[inner], column(0, d), None, False)
+        sinkb[inner] = piece[...]
+    sent("f3", sinkb.at[0:ni - 1])
 
     def relay(o):
+        @pl.when(down(o))
         def _():
             arrived(f"w{o}", buf.at[o, par])
             copy(f"r{o}", buf.at[o, par], buf.at[o, par], across).start()
-        when(down(o), _)
-
-    def relays(order):
-        def _():
-            for o in order:
-                relay(o)
-        return _
-
-    near = list(range(1, FAR))
-    when(outer == 0, relays(near[::-1]))
-    when(outer == no - 1, relays(near))
-    when((outer != 0) & (outer != no - 1), relays(near[::2] + near[1::2]))
-    for o in near:
+
+    slot(0)()
+
+    @pl.when(top)
+    def _():
+        spread()
+        relay(2)
+        relay(1)
+
+    @pl.when(outer != 0)
+    def _():
+        relay(1)
+        relay(2)
+        arrived("f2", piece)
+        spread()
+    for o in (1, 2):
         pending.append((down(o), copy(f"r{o}", buf.at[o, par], buf.at[o, par], across)))
-
-    @pl.when(outer != 0)
-    def _():
-        arrived("f2", piece)
-    for d in range(1, ni):
-        start("f3", piece, sinkb.at[inner], column(0, d), None, False)
-    sent("f3", sinkb.at[0:ni - 1])
-    sinkb[inner] = piece[...]
 
     @pl.when(down(FAR))
     def _():
@@ -260,12 +303,18 @@
         arrived("w4x", buf.at[FAR, other])
         slot(FAR)()
 
-    for o in near:
+    @pl.when(down(DIRECT))
+    def _():
+        arrived(f"w{DIRECT}", buf.at[DIRECT])
+        slot(DIRECT)()
+
+    def last(o):
         @pl.when(down(o))
         def _():
             arrived(f"r{o}", buf.at[o, other])
             slot(o)()
 
+    last(1)
     arrived("f3", sinkb.at[0:ni - 1])
 
     @pl.when(b >= 1)
@@ -275,6 +324,8 @@
         keys = jnp.concatenate(a[0:cut] + a[ni:ni + cut], 0)
         vals = jnp.concatenate(a[cut:ni] + a[ni + cut:], 0)
         scores_of(keys, vals, STEPS, jk < sink_end)
+
+    last(2)
 
     high = run[0:1]
     scale = 1.0 / run[1:2]
@@ -330,8 +381,17 @@
             gout[o] = mine[o] + xin[o]
         start(f"gz{o}", gout.at[o], gin.at[o], seq(-o), down(o))
 
-    give_near(3)
+    @pl.when(down(DIRECT))
+    def _():
+        keep, give = grads(DIRECT)
+        g3out[0] = keep
+        g3out[1] = give
+    for p, device in enumerate(both(-DIRECT)):
+        start("g3", g3out.at[p], g3in.at[p], device, down(DIRECT), False)
+    sent("g3", g3out, down(DIRECT))
+
     give_near(2)
+    give_near(1)
 
     @pl.when(down(FAR))
     def _():
@@ -339,7 +399,10 @@
         g4out[0] = keep
         g4out[1] = give
     start("g4", g4out, g4in, seq(-FAR), down(FAR))
-    give_near(1)
+
+    keep, give = grads(0)
+    mine[0] = keep
+    xout[0] = give
 
     where = pl.ds(pl.multiple_of(inner * pr, pr), pr)
     arrived("b1", sin.at[1:2 * ni])
@@ -354,10 +417,6 @@
                 start("b2", s2, s2in.at[i * no + z], (head, 0, 0), mine_here, False)
     sent("b2", s2, jnp.logical_not(first))
 
-    pass_on(3)
-    keep, give = grads(0)
-    mine[0] = keep
-    xout[0] = give
     pass_on(2)
 
     @pl.when(up(FAR))
@@ -381,7 +440,12 @@
 
     arrived("gx0", xin.at[0])
     dkv_ref[...] = mine[0] + xin[0]
-    for o in range(FAR - 1, 0, -1):
+
+    @pl.when(up(DIRECT))
+    def _():
+        arrived("g3", g3in)
+        dkv_ref[...] += g3in[0] + g3in[1]
+    for o in (2, 1):
         @pl.when(up(o))
         def _():
             arrived(f"gz{o}", gin.at[o])
@@ -420,7 +484,7 @@
     codes = block_codes.T
     pr = block // ni
     total = STEPS + 1
-    sems = 23
+    sems = 21
     vmem, hbm = pl.BlockSpec(memory_space=pltpu.VMEM), pl.BlockSpec(memory_space=pltpu.HBM)
     tile = (block, dim)
     grad_q, grad_kv = pl.pallas_call(
@@ -449,11 +513,11 @@
             pltpu.VMEM((8, rows), f32),
             pltpu.VMEM((total, 2, block, rows), bf16),
             pltpu.VMEM((total, dim, 3 * block), bf16),
-            pltpu.VMEM((FAR,) + tile, f32),
-            pltpu.VMEM((FAR,) + tile, f32),
-            pltpu.VMEM((FAR,) + tile, f32),
-            pltpu.VMEM((FAR,) + tile, f32),
-            pltpu.VMEM((FAR,) + tile, f32),
+            pltpu.VMEM((DIRECT,) + tile, f32),
+            pltpu.VMEM((DIRECT,) + tile, f32),
+            pltpu.VMEM((DIRECT,) + tile, f32),
+            pltpu.VMEM((DIRECT,) + tile, f32),
+            pltpu.VMEM((DIRECT,) + tile, f32),
             pltpu.VMEM((2,) + tile, f32),
             pltpu.VMEM((2,) + tile, f32),
             pltpu.VMEM((2,) + tile, f32),
@@ -461,8 +525,11 @@
             pltpu.VMEM((pr, dim), f32),
             pltpu.VMEM((ni * no, pr, dim), f32),
             pltpu.VMEM((dim, rows), f32),
+            pltpu.VMEM((2,) + tile, f32),
+            pltpu.VMEM((2,) + tile, f32),
             pltpu.SemaphoreType.DMA((sems,)),
             pltpu.SemaphoreType.DMA((sems,)),
+            pltpu.SemaphoreType.REGULAR((FAR,)),
         ],
         compiler_params=pltpu.CompilerParams(
             collective_id=0, has_side_effects=True, vmem_limit_bytes=66_000_000

time: 34.7 us -> 32.9 us (0.948)
  Pallas kernels: 32.6 us -> 30.8 us
    pallas_call x1, Pallas kernels: 31.9 us -> 30.1 us  [shards(): pl.pallas_call(functools.partial(kernel, (ni, no, heads_dev)), out_shape=...]
where the time goes in v2:
time: 32.9 us; the launch traced here: 32.8 us
  Pallas kernels  30.8 us (94%)
  between operations  1.93 us (6%)
    pallas_call x1, Pallas kernels, shards(): pl.pallas_call(functools.partial(kernel, (ni, no, heads_dev)), out_shape=...  30.1 us
    pallas_call x1, Pallas kernels, shards(): pl.pallas_call(store, out_shape=(jax.ShapeDtypeStruct((rows, dim), f32),...  0.74 us

profile of v2, /device:TPU:0, one launch (start us, length us, event | category | flops | bytes accessed | tf_op | source)
XLA Modules:
  0.0 32.8 jit_solution(4331296602841172088)
XLA Ops:
  1.9 30.1 %shard_map.94 = (f32[512,128]{1,0:T(8,128)S(1)}, f32[128,128]{1,0:T(8,128)S(1)}) custom-call(s32[1]{0:T(128)S(6)} %copy.10.sink_hbm, s32[1]{0:T(128)S(6)} %copy.11.window_hbm, s32[5,16]{1,0:T(8,128)} %bitcast.12, f32[512,128]{1,0:T(8,128)} %bitcast.8, f32[64,128]{1,0:T(8,128)} %bitcast.10, f32[64,128]{1,0:T(8,128)} %bitcast.11, f32[512,128]{1,0:T(8,128)} %bitcast.9), custom_call_target="tpu_custom_call" | custom-call | tf_op jit(solution)/shard_map/pallas_call | solution.py:490
  32.0 0.7 %shard_map.95 = (f32[512,128]{1,0:T(8,128)}, f32[64,128]{1,0:T(8,128)}, f32[64,128]{1,0:T(8,128)}) custom-call(f32[512,128]{1,0:T(8,128)S(1)} %get-tuple-element.8.dq_ref, f32[128,128]{1,0:T(8,128)S(1)} %get-tuple-element.9.dkv_ref), custom_call_target="tpu_custom_call" | custom-call | tf_op jit(solution)/shard_map/pallas_call | solution.py:541

commit v3 on v2

--- a/solution.py
+++ b/solution.py
@@ -12,6 +12,7 @@
 FAR = STEPS - 1
 DIRECT = FAR - 1
 LATE = (2, 3)
+ROOT = (1,)
 BIG = 1 << 28
 very_low = -1e30
 f32, bf16 = jnp.float32, jnp.bfloat16
@@ -40,7 +41,7 @@
     sizes, sink_hbm, window_hbm, codes_hbm, q_hbm, k_hbm, v_hbm, g_hbm, dq_ref, dkv_ref,
     sink_ref, window_ref, codes_ref, q_ref, g_ref, load, buf, sinkb, piece, qcat, gcat,
     st, dp, peak, run, ds, ktcat, xout, xin, mine, gout, gin, g4out, g4in, sg, sin, s2, s2in,
-    dqt, g3out, g3in, send, recv, late,
+    dqt, g3out, g3in, gdin, send, recv, late,
 ):
     ni, no, heads_dev = sizes
     half, block = k_hbm.shape
@@ -79,14 +80,15 @@
 
     pending = []
 
-    def copy(name, src, dst, device):
+    def copy(name, src, dst, device, via=None):
         return pltpu.make_async_remote_copy(
-            src_ref=src, dst_ref=dst, send_sem=send.at[sem(name)], recv_sem=recv.at[sem(name)],
+            src_ref=src, dst_ref=dst,
+            send_sem=send.at[sem(via or name)], recv_sem=recv.at[sem(name)],
             device_id=device, device_id_type=MESH,
         )
 
-    def start(name, src, dst, device, cond=None, sent=True):
-        c = copy(name, src, dst, device)
+    def start(name, src, dst, device, cond=None, sent=True, via=None):
+        c = copy(name, src, dst, device, via)
         when(cond, c.start)
         if sent:
             pending.append((cond, c))
@@ -109,56 +111,51 @@
     def signal(where, device):
         pl.semaphore_signal(where, inc=1, device_id=device, device_id_type=MESH)
 
-    def late_up(o):
-        return outer + o < no
-
-    def late_down(o):
-        return outer >= o
-
-    def one(cond, n=1):
-        return jnp.where(cond, n, 0)
+    end = outer == no - 1
 
     def both(o):
         head_o, inner_o, outer_o = seq(o)
         return [(head, inner_o, outer_o), (partner, inner_o, outer_o)]
 
+    def one(cond, n=1):
+        return jnp.where(cond, n, 0)
+
+    far = outer >= 2
+    bridged = (lax.rem(inner, 2) == 0) & (inner > 0)
+    bridge = far & bridged
+
+    def sends(o):
+        if o == 2:
+            return up(o) & (top | ((outer + o >= no) & (lax.rem(inner, 2) == 0)))
+        return up(o)
+
+    def hears(o):
+        if o == 2:
+            return down(o) & ((outer == o) | ((outer < o) & (lax.rem(inner, 2) == 1)))
+        return down(o)
+
     signal(barrier, across)
     for d in range(1, ni):
         signal(barrier, column(0, d))
+    expect = ni + one(first, ni - 1)
     when(top & (inner != 0), lambda: signal(barrier, (partner, 0, 0)))
-    expect = ni + one(first, ni - 1)
     for o in range(1, STEPS):
-        early = down(o)
-        soon = up(o)
+        asks, tells = sends(o), hears(o)
         if o in LATE:
-            early = early & jnp.logical_not(late_down(o))
-            soon = soon & jnp.logical_not(late_up(o))
-
-            @pl.when(late_up(o))
-            def _():
-                for device in both(o)[:1 + (o == DIRECT)]:
-                    signal(barrier, device)
-            expect = expect + one(late_down(o), 1 + (o == DIRECT))
-
-        @pl.when(early)
-        def _():
-            for device in both(-o)[:1 + (o == DIRECT)]:
-                signal(barrier, device)
-        expect = expect + one(soon, 1 + (o == DIRECT))
+            asks, tells = asks & (outer != 0), tells & (outer != o)
+        when(tells, lambda: signal(barrier, seq(-o)))
+        expect = expect + one(asks)
+    for o in LATE:
+        when(top, lambda: signal(barrier, seq(o)))
+    near_bridge = (outer < 2) & bridged
+    when(near_bridge, lambda: signal(barrier, seq(2)))
+    expect = expect + one(far) + one(bridge)
 
     for x in loads:
         x.start()
     pl.semaphore_wait(barrier, expect)
-    for o in LATE:
-        @pl.when(late_down(o))
-        def _():
-            for device in both(-o)[:1 + (o == DIRECT)]:
-                signal(late.at[o], device)
-
-    def entered(o):
-        @pl.when(late_up(o))
-        def _():
-            pl.semaphore_wait(late.at[o], 1 + (o == DIRECT))
+    for i, o in enumerate(LATE):
+        when(outer == o, lambda: signal(late.at[i], seq(-o)))
 
     def own_to(name, dst, devices, cond=None):
         for device in devices:
@@ -179,9 +176,10 @@
 
     own_to("x0", buf.at[0, par], [across])
     sent("x0", buf.at[0, 0])
-    for o in (1, FAR):
-        own_to(f"w{o}", buf.at[o, par], [seq(o)], up(o))
-        sent(f"w{o}", buf.at[0, 0], up(o))
+    for o in range(1, STEPS):
+        sent(f"w{o}", buf.at[0, 0], sends(o))
+        now = sends(o) & (outer != 0) if o in LATE else sends(o)
+        own_to(f"w{o}", buf.at[o, par], [seq(o)], now)
 
     loads[2].wait()
     q0, q1 = two(q_ref[...])
@@ -247,25 +245,44 @@
             )
         return _
 
-    entered(2)
-    own_to("w2", buf.at[2, par], [seq(2)], up(2))
-    sent("w2", buf.at[0, 0], up(2))
+    def relay(o):
+        @pl.when(down(o))
+        def _():
+            arrived(f"w{o}", buf.at[o, par])
+            copy(f"r{o}", buf.at[o, par], buf.at[o, par], across).start()
 
     @pl.when(top)
     def _():
+        pl.semaphore_wait(late.at[0], 1)
+        own_to("w2", buf.at[2, par], [seq(2)])
+
         @pl.when(jnp.logical_not(first))
         def _():
             arrived("f1_0", piece.at[par])
         arrived("f1_1", piece.at[other])
-    start("f2", piece, piece, (head, inner, 1), top, False)
-    entered(DIRECT)
-    for z in range(2, no):
-        start("f2", piece, piece, (head, inner, z), top, False)
+        start("f2", piece, piece, (head, inner, 1), None, False)
+        pl.semaphore_wait(late.at[1], 1)
+        for z in range(no - 1, 1, -1):
+            start("f2", piece, piece, (head, inner, z), None, False)
+        own_to("w3", buf.at[3, par], [seq(3)])
     sent("f2", sinkb.at[0:no - 1], top)
-    own_to(f"w{DIRECT}", buf.at[DIRECT, par], both(DIRECT), up(DIRECT))
-    sent(f"w{DIRECT}", buf.at[0], up(DIRECT))
+
+    @pl.when(outer != 0)
+    def _():
+        relay(1)
+
+    between = outer == no - 2
+    start("w2", buf.at[1, par], buf.at[2, par], seq(1), between, False, "on")
+    pending.append((between, copy("w2", buf.at[1, par], buf.at[2, par], across, "on")))
+
+    @pl.when(bridge)
+    def _():
+        arrived(f"w{FAR}", buf.at[FAR, par])
+    start("w2", buf.at[FAR, par], buf.at[2, par], seq(-2), bridge, False, "over")
+    pending.append((bridge, copy("w2", buf.at[FAR, par], buf.at[2, par], across, "over")))
 
     arrived("x0", buf.at[0, other])
+    start("w3x", buf.at[0, other], buf.at[3, other], seq(3), up(3))
     start("w4x", buf.at[0, other], buf.at[FAR, other], seq(FAR), up(FAR))
 
     def spread():
@@ -274,58 +291,98 @@
         sinkb[inner] = piece[...]
     sent("f3", sinkb.at[0:ni - 1])
 
-    def relay(o):
-        @pl.when(down(o))
-        def _():
-            arrived(f"w{o}", buf.at[o, par])
-            copy(f"r{o}", buf.at[o, par], buf.at[o, par], across).start()
-
-    slot(0)()
-
-    @pl.when(top)
-    def _():
-        spread()
-        relay(2)
-        relay(1)
-
-    @pl.when(outer != 0)
-    def _():
-        relay(1)
-        relay(2)
+    def sink():
         arrived("f2", piece)
         spread()
+
+    slot(0)()
+
+    @pl.when(top)
+    def _():
+        spread()
+
+        @pl.when(bridged)
+        def _():
+            relay(1)
+            relay(2)
+
+        @pl.when(jnp.logical_not(bridged))
+        def _():
+            relay(2)
+            relay(1)
+
+    @pl.when(outer == 1)
+    def _():
+        sink()
+        relay(2)
+
+    @pl.when(outer > 1)
+    def _():
+        relay(2)
+        sink()
     for o in (1, 2):
         pending.append((down(o), copy(f"r{o}", buf.at[o, par], buf.at[o, par], across)))
 
     @pl.when(down(FAR))
     def _():
-        arrived(f"w{FAR}", buf.at[FAR, par])
+        @pl.when(jnp.logical_not(bridge))
+        def _():
+            arrived(f"w{FAR}", buf.at[FAR, par])
         arrived("w4x", buf.at[FAR, other])
         slot(FAR)()
 
-    @pl.when(down(DIRECT))
-    def _():
-        arrived(f"w{DIRECT}", buf.at[DIRECT])
-        slot(DIRECT)()
-
     def last(o):
         @pl.when(down(o))
         def _():
             arrived(f"r{o}", buf.at[o, other])
             slot(o)()
 
-    last(1)
-    arrived("f3", sinkb.at[0:ni - 1])
-
-    @pl.when(b >= 1)
-    def _():
-        a = [sinkb[i, p] for p in range(2) for i in range(ni)]
-        cut = ni // 2
-        keys = jnp.concatenate(a[0:cut] + a[ni:ni + cut], 0)
-        vals = jnp.concatenate(a[cut:ni] + a[ni + cut:], 0)
-        scores_of(keys, vals, STEPS, jk < sink_end)
-
-    last(2)
+    def sinks():
+        arrived("f3", sinkb.at[0:ni - 1])
+
+        @pl.when(b >= 1)
+        def _():
+            a = [sinkb[i, p] for p in range(2) for i in range(ni)]
+            cut = ni // 2
+            keys = jnp.concatenate(a[0:cut] + a[ni:ni + cut], 0)
+            vals = jnp.concatenate(a[cut:ni] + a[ni + cut:], 0)
+            scores_of(keys, vals, STEPS, jk < sink_end)
+
+    def third():
+        @pl.when(down(3))
+        def _():
+            arrived("w3", buf.at[3, par])
+            arrived("w3x", buf.at[3, other])
+            slot(3)()
+
+    @pl.when(top)
+    def _():
+        third()
+        sinks()
+
+        @pl.when(bridged)
+        def _():
+            last(1)
+            last(2)
+
+        @pl.when(jnp.logical_not(bridged))
+        def _():
+            last(2)
+            last(1)
+
+    @pl.when((outer != 0) & jnp.logical_not(end))
+    def _():
+        third()
+        last(1)
+        last(2)
+        sinks()
+
+    @pl.when(end)
+    def _():
+        last(1)
+        last(2)
+        sinks()
+        third()
 
     high = run[0:1]
     scale = 1.0 / run[1:2]
@@ -350,6 +407,40 @@
         give = jnp.where(par == 0, odd, even)
         return keep, give
 
+    def at_root(o):
+        return b == (o if o in ROOT else -1)
+
+    def give_near(o):
+        @pl.when(down(o))
+        def _():
+            keep, give = grads(o)
+            mine[o] = keep
+            xout[o] = give
+        c = copy(f"gx{o}", xout.at[o], xin.at[o], across)
+        when(down(o) & (~at_root(o)), c.start)
+        if o not in ROOT:
+            return
+        start(f"gd{o}", mine.at[o], gdin.at[o - 1, 0], (head, 0, 0), at_root(o), False)
+        start(f"gd{o}", xout.at[o], gdin.at[o - 1, 1], (partner, 0, 0), at_root(o), False)
+        sent(f"gd{o}", g3out, at_root(o))
+
+    def pass_on(o):
+        @pl.when(down(o) & (~at_root(o)))
+        def _():
+            arrived(f"gx{o}", xin.at[o])
+            gout[o] = mine[o] + xin[o]
+        c = copy(f"gz{o}", gout.at[o], gin.at[o], seq(-o))
+        when(down(o) & (~at_root(o)), c.start)
+
+    for o in (1, 2):
+        for name in ("gx", "gz"):
+            c = copy(f"{name}{o}", xout.at[o], xin.at[o], across)
+            pending.append((down(o) & (~at_root(o)), c))
+
+    @pl.when(outer == 2)
+    def _():
+        give_near(2)
+
     @pl.when(b >= 1)
     def _():
         keep, give = grads(STEPS)
@@ -360,37 +451,25 @@
     def _():
         sg[...] = jnp.zeros_like(sg)
 
-    for p, d in columns:
+    for p, d in columns[::-1]:
         target = lax.rem(inner + d, ni)
         rng = pl.ds(pl.multiple_of(target * pr, pr), pr)
         start("b1", sg.at[p, rng], sin.at[p * ni + d], column(p, d), None, False)
     sent("b1", sin.at[1:2 * ni])
 
-    def give_near(o):
-        @pl.when(down(o))
-        def _():
-            keep, give = grads(o)
-            mine[o] = keep
-            xout[o] = give
-        start(f"gx{o}", xout.at[o], xin.at[o], across, down(o))
-
-    def pass_on(o):
-        @pl.when(down(o))
-        def _():
-            arrived(f"gx{o}", xin.at[o])
-            gout[o] = mine[o] + xin[o]
-        start(f"gz{o}", gout.at[o], gin.at[o], seq(-o), down(o))
-
-    @pl.when(down(DIRECT))
-    def _():
-        keep, give = grads(DIRECT)
+    @pl.when(down(3))
+    def _():
+        keep, give = grads(3)
         g3out[0] = keep
         g3out[1] = give
-    for p, device in enumerate(both(-DIRECT)):
-        start("g3", g3out.at[p], g3in.at[p], device, down(DIRECT), False)
-    sent("g3", g3out, down(DIRECT))
-
-    give_near(2)
+    for p, device in enumerate(both(-3)):
+        start("g3", g3out.at[p], g3in.at[p], device, down(3) & end if p else down(3), False)
+    start("g3", g3out.at[1], g3in.at[1], seq(-3), down(3) & jnp.logical_not(end), False)
+    sent("g3", g3out, down(3))
+
+    @pl.when(outer != 2)
+    def _():
+        give_near(2)
     give_near(1)
 
     @pl.when(down(FAR))
@@ -405,6 +484,9 @@
     xout[0] = give
 
     where = pl.ds(pl.multiple_of(inner * pr, pr), pr)
+    @pl.when(outer == 2)
+    def _():
+        pass_on(2)
     arrived("b1", sin.at[1:2 * ni])
     acc = sg[0, where]
     for p, d in columns:
@@ -417,15 +499,21 @@
                 start("b2", s2, s2in.at[i * no + z], (head, 0, 0), mine_here, False)
     sent("b2", s2, jnp.logical_not(first))
 
-    pass_on(2)
-
-    @pl.when(up(FAR))
-    def _():
-        arrived("g4", g4in)
-        mine[0] += g4in[0]
-        xout[0] += g4in[1]
+    @pl.when(outer != 2)
+    def _():
+        pass_on(2)
+    pass_on(1)
+
+    def join(cond, name, ref):
+        @pl.when(cond)
+        def _():
+            arrived(name, ref)
+            mine[0] += ref[0]
+            xout[0] += ref[1]
+
+    join(up(FAR), "g4", g4in)
+    join(up(3) & jnp.logical_not(top), "g3", g3in)
     start("gx0", xout.at[0], xin.at[0], across)
-    pass_on(1)
 
     def dq_part(i):
         hi = ds[i, 0]
@@ -441,12 +529,18 @@
     arrived("gx0", xin.at[0])
     dkv_ref[...] = mine[0] + xin[0]
 
-    @pl.when(up(DIRECT))
+
+    @pl.when(up(3) & top)
     def _():
         arrived("g3", g3in)
         dkv_ref[...] += g3in[0] + g3in[1]
+    for o in ROOT:
+        @pl.when(first)
+        def _():
+            arrived(f"gd{o}", gdin.at[o - 1])
+            dkv_ref[...] += gdin[o - 1, 0] + gdin[o - 1, 1]
     for o in (2, 1):
-        @pl.when(up(o))
+        @pl.when(up(o) & jnp.logical_not(first) if o in ROOT else up(o))
         def _():
             arrived(f"gz{o}", gin.at[o])
             dkv_ref[...] += gin[o]
@@ -484,7 +578,7 @@
     codes = block_codes.T
     pr = block // ni
     total = STEPS + 1
-    sems = 21
+    sems = 26
     vmem, hbm = pl.BlockSpec(memory_space=pltpu.VMEM), pl.BlockSpec(memory_space=pltpu.HBM)
     tile = (block, dim)
     grad_q, grad_kv = pl.pallas_call(
@@ -527,9 +621,10 @@
             pltpu.VMEM((dim, rows), f32),
             pltpu.VMEM((2,) + tile, f32),
             pltpu.VMEM((2,) + tile, f32),
+            pltpu.VMEM((2, 2) + tile, f32),
             pltpu.SemaphoreType.DMA((sems,)),
             pltpu.SemaphoreType.DMA((sems,)),
-            pltpu.SemaphoreType.REGULAR((FAR,)),
+            pltpu.SemaphoreType.REGULAR((2,)),
         ],
         compiler_params=pltpu.CompilerParams(
             collective_id=0, has_side_effects=True, vmem_limit_bytes=66_000_000

time: 32.9 us -> 29.8 us (0.906)
  Pallas kernels: 30.8 us -> 27.7 us
    pallas_call x1, Pallas kernels: 30.1 us -> 26.9 us  [shards(): pl.pallas_call(functools.partial(kernel, (ni, no, heads_dev)), out_shape=...]
where the time goes in v3:
time: 29.8 us; the launch traced here: 29.6 us
  Pallas kernels  27.7 us (93%)
  between operations  1.93 us (6%)
    pallas_call x1, Pallas kernels, shards(): pl.pallas_call(functools.partial(kernel, (ni, no, heads_dev)), out_shape=...  26.9 us
    pallas_call x1, Pallas kernels, shards(): pl.pallas_call(store, out_shape=(jax.ShapeDtypeStruct((rows, dim), f32),...  0.74 us

profile of v3, /device:TPU:0, one launch (start us, length us, event | category | flops | bytes accessed | tf_op | source)
XLA Modules:
  0.0 29.6 jit_solution(15843271911516126427)
XLA Ops:
  1.9 26.9 %shard_map.94 = (f32[512,128]{1,0:T(8,128)S(1)}, f32[128,128]{1,0:T(8,128)S(1)}) custom-call(s32[1]{0:T(128)S(6)} %copy.10.sink_hbm, s32[1]{0:T(128)S(6)} %copy.11.window_hbm, s32[5,16]{1,0:T(8,128)} %bitcast.12, f32[512,128]{1,0:T(8,128)} %bitcast.8, f32[64,128]{1,0:T(8,128)} %bitcast.10, f32[64,128]{1,0:T(8,128)} %bitcast.11, f32[512,128]{1,0:T(8,128)} %bitcast.9), custom_call_target="tpu_custom_call" | custom-call | tf_op jit(solution)/shard_map/pallas_call | solution.py:584
  28.9 0.7 %shard_map.95 = (f32[512,128]{1,0:T(8,128)}, f32[64,128]{1,0:T(8,128)}, f32[64,128]{1,0:T(8,128)}) custom-call(f32[512,128]{1,0:T(8,128)S(1)} %get-tuple-element.8.dq_ref, f32[128,128]{1,0:T(8,128)S(1)} %get-tuple-element.9.dkv_ref), custom_call_target="tpu_custom_call" | custom-call | tf_op jit(solution)/shard_map/pallas_call | solution.py:636

commit v4 on v3

--- a/solution.py
+++ b/solution.py
@@ -15,6 +15,12 @@
 ROOT = (1,)
 BIG = 1 << 28
 very_low = -1e30
+SENT = {
+    "x0": "all", "f3": "all", "b1": "all", "gx0": "all", "w3x": "w3", "w4x": "w4",
+    "r1": "d1", "gx1": "d1", "gz1": "d1", "gd1": "d1", "r2": "d2", "gx2": "d2", "gz2": "d2",
+    "f1_0": "f1", "f1_1": "f1",
+}
+CAME = {"w3x": "w3", "f1_0": "f1", "f1_1": "f1"}
 f32, bf16 = jnp.float32, jnp.bfloat16
 MESH = pl.DeviceIdType.MESH
 NT = (((1,), (1,)), ((), ()))
@@ -41,7 +47,7 @@
     sizes, sink_hbm, window_hbm, codes_hbm, q_hbm, k_hbm, v_hbm, g_hbm, dq_ref, dkv_ref,
     sink_ref, window_ref, codes_ref, q_ref, g_ref, load, buf, sinkb, piece, qcat, gcat,
     st, dp, peak, run, ds, ktcat, xout, xin, mine, gout, gin, g4out, g4in, sg, sin, s2, s2in,
-    dqt, g3out, g3in, gdin, send, recv, late,
+    dqt, g3out, g3in, gdin, tally, send, recv, late,
 ):
     ni, no, heads_dev = sizes
     half, block = k_hbm.shape
@@ -73,31 +79,28 @@
     def down(o):
         return b >= o
 
-    slots = {}
-
-    def sem(name):
-        return slots.setdefault(name, len(slots))
-
-    pending = []
+    sent_slots, slots = {}, {}
+
+    def numbered(table, name):
+        return table.setdefault(name, len(table))
 
     def copy(name, src, dst, device, via=None):
+        out = numbered(sent_slots, SENT.get(via or name, via or name))
         return pltpu.make_async_remote_copy(
             src_ref=src, dst_ref=dst,
-            send_sem=send.at[sem(via or name)], recv_sem=recv.at[sem(name)],
+            send_sem=send.at[out], recv_sem=recv.at[numbered(slots, CAME.get(name, name))],
             device_id=device, device_id_type=MESH,
         )
 
-    def start(name, src, dst, device, cond=None, sent=True, via=None):
-        c = copy(name, src, dst, device, via)
-        when(cond, c.start)
-        if sent:
-            pending.append((cond, c))
-
-    def sent(name, like, cond=None):
-        pending.append((cond, copy(name, like, like, across)))
+    def start(name, src, dst, device, cond=None, via=None):
+        when(cond, copy(name, src, dst, device, via).start)
 
     def arrived(name, dst):
-        copy(name, dst, dst, across).wait_recv()
+        pltpu.make_async_remote_copy(
+            src_ref=dst, dst_ref=dst, send_sem=send.at[0],
+            recv_sem=recv.at[numbered(slots, CAME.get(name, name))],
+            device_id=across, device_id_type=MESH,
+        ).wait_recv()
 
     moves = [
         (k_hbm, buf.at[0, par, 0:half]), (v_hbm, buf.at[0, par, half:2 * half]),
@@ -159,8 +162,8 @@
 
     def own_to(name, dst, devices, cond=None):
         for device in devices:
-            start(name, k_hbm, dst.at[0:half], device, cond, False)
-            start(name, v_hbm, dst.at[half:2 * half], device, cond, False)
+            start(name, k_hbm, dst.at[0:half], device, cond)
+            start(name, v_hbm, dst.at[half:2 * half], device, cond)
 
     def rows_of(i):
         return (k_hbm.at[pl.ds(i * pr, pr)] if i * pr < half
@@ -170,14 +173,10 @@
         for p in range(2):
             if i or p:
                 to = (partner if p else head, i, 0)
-                start(f"f1_{p}", rows_of(i), piece.at[par], to, first, False)
-    sent("f1_0", buf.at[0, 0, 0:(ni - 1) * pr], first)
-    sent("f1_1", buf.at[0, 0], first)
+                start(f"f1_{p}", rows_of(i), piece.at[par], to, first)
 
     own_to("x0", buf.at[0, par], [across])
-    sent("x0", buf.at[0, 0])
     for o in range(1, STEPS):
-        sent(f"w{o}", buf.at[0, 0], sends(o))
         now = sends(o) & (outer != 0) if o in LATE else sends(o)
         own_to(f"w{o}", buf.at[o, par], [seq(o)], now)
 
@@ -258,28 +257,28 @@
 
         @pl.when(jnp.logical_not(first))
         def _():
-            arrived("f1_0", piece.at[par])
-        arrived("f1_1", piece.at[other])
-        start("f2", piece, piece, (head, inner, 1), None, False)
+            arrived("f1", piece)
+
+        @pl.when(first)
+        def _():
+            arrived("f1", piece.at[other])
+        start("f2", piece, piece, (head, inner, 1))
         pl.semaphore_wait(late.at[1], 1)
         for z in range(no - 1, 1, -1):
-            start("f2", piece, piece, (head, inner, z), None, False)
+            start("f2", piece, piece, (head, inner, z))
         own_to("w3", buf.at[3, par], [seq(3)])
-    sent("f2", sinkb.at[0:no - 1], top)
 
     @pl.when(outer != 0)
     def _():
         relay(1)
 
     between = outer == no - 2
-    start("w2", buf.at[1, par], buf.at[2, par], seq(1), between, False, "on")
-    pending.append((between, copy("w2", buf.at[1, par], buf.at[2, par], across, "on")))
+    start("w2", buf.at[1, par], buf.at[2, par], seq(1), between, "on")
 
     @pl.when(bridge)
     def _():
         arrived(f"w{FAR}", buf.at[FAR, par])
-    start("w2", buf.at[FAR, par], buf.at[2, par], seq(-2), bridge, False, "over")
-    pending.append((bridge, copy("w2", buf.at[FAR, par], buf.at[2, par], across, "over")))
+    start("w2", buf.at[FAR, par], buf.at[2, par], seq(-2), bridge, "over")
 
     arrived("x0", buf.at[0, other])
     start("w3x", buf.at[0, other], buf.at[3, other], seq(3), up(3))
@@ -287,9 +286,8 @@
 
     def spread():
         for d in range(1, ni):
-            start("f3", piece, sinkb.at[inner], column(0, d), None, False)
+            start("f3", piece, sinkb.at[inner], column(0, d))
         sinkb[inner] = piece[...]
-    sent("f3", sinkb.at[0:ni - 1])
 
     def sink():
         arrived("f2", piece)
@@ -320,8 +318,6 @@
     def _():
         relay(2)
         sink()
-    for o in (1, 2):
-        pending.append((down(o), copy(f"r{o}", buf.at[o, par], buf.at[o, par], across)))
 
     @pl.when(down(FAR))
     def _():
@@ -351,8 +347,7 @@
     def third():
         @pl.when(down(3))
         def _():
-            arrived("w3", buf.at[3, par])
-            arrived("w3x", buf.at[3, other])
+            arrived("w3", buf.at[3])
             slot(3)()
 
     @pl.when(top)
@@ -420,9 +415,8 @@
         when(down(o) & (~at_root(o)), c.start)
         if o not in ROOT:
             return
-        start(f"gd{o}", mine.at[o], gdin.at[o - 1, 0], (head, 0, 0), at_root(o), False)
-        start(f"gd{o}", xout.at[o], gdin.at[o - 1, 1], (partner, 0, 0), at_root(o), False)
-        sent(f"gd{o}", g3out, at_root(o))
+        start(f"gd{o}", mine.at[o], gdin.at[o - 1, 0], (head, 0, 0), at_root(o))
+        start(f"gd{o}", xout.at[o], gdin.at[o - 1, 1], (partner, 0, 0), at_root(o))
 
     def pass_on(o):
         @pl.when(down(o) & (~at_root(o)))
@@ -432,11 +426,6 @@
         c = copy(f"gz{o}", gout.at[o], gin.at[o], seq(-o))
         when(down(o) & (~at_root(o)), c.start)
 
-    for o in (1, 2):
-        for name in ("gx", "gz"):
-            c = copy(f"{name}{o}", xout.at[o], xin.at[o], across)
-            pending.append((down(o) & (~at_root(o)), c))
-
     @pl.when(outer == 2)
     def _():
         give_near(2)
@@ -454,8 +443,7 @@
     for p, d in columns[::-1]:
         target = lax.rem(inner + d, ni)
         rng = pl.ds(pl.multiple_of(target * pr, pr), pr)
-        start("b1", sg.at[p, rng], sin.at[p * ni + d], column(p, d), None, False)
-    sent("b1", sin.at[1:2 * ni])
+        start("b1", sg.at[p, rng], sin.at[p * ni + d], column(p, d))
 
     @pl.when(down(3))
     def _():
@@ -463,9 +451,8 @@
         g3out[0] = keep
         g3out[1] = give
     for p, device in enumerate(both(-3)):
-        start("g3", g3out.at[p], g3in.at[p], device, down(3) & end if p else down(3), False)
-    start("g3", g3out.at[1], g3in.at[1], seq(-3), down(3) & jnp.logical_not(end), False)
-    sent("g3", g3out, down(3))
+        start("g3", g3out.at[p], g3in.at[p], device, down(3) & end if p else down(3))
+    start("g3", g3out.at[1], g3in.at[1], seq(-3), down(3) & jnp.logical_not(end))
 
     @pl.when(outer != 2)
     def _():
@@ -496,8 +483,7 @@
         for z in range(no):
             if i or z:
                 mine_here = (inner == i) & (outer == z)
-                start("b2", s2, s2in.at[i * no + z], (head, 0, 0), mine_here, False)
-    sent("b2", s2, jnp.logical_not(first))
+                start("b2", s2, s2in.at[i * no + z], (head, 0, 0), mine_here)
 
     @pl.when(outer != 2)
     def _():
@@ -554,9 +540,23 @@
                 part = part + s2in[i * no + z]
             dkv_ref[i * pr:(i + 1) * pr] += part
 
-    for cond, c in pending:
-        when(cond, c.wait_send)
-    assert len(slots) <= send.shape[0], len(slots)
+    one_tile = buf.at[0, 0]
+    waits = [
+        (None, "all", tally), (up(1), "w1", one_tile), (sends(2), "w2", one_tile),
+        (up(3), "w3", buf.at[0]), (up(FAR), "w4", buf.at[0]),
+        (down(1), "d1", xout.at[0:3]), (down(2), "d2", xout.at[0:3]),
+        (down(3), "g3", g3out), (down(FAR), "g4", g4out),
+        (top, "f2", sinkb.at[0:no - 1]), (first, "f1", sin.at[1:2 * ni]),
+        (jnp.logical_not(first), "b2", s2),
+        (between, "on", one_tile), (bridge, "over", one_tile),
+    ]
+    assert {w[1] for w in waits} == set(sent_slots), sent_slots
+    for cond, name, like in waits:
+        when(cond, pltpu.make_async_remote_copy(
+            src_ref=like, dst_ref=like, send_sem=send.at[sent_slots[name]], recv_sem=recv.at[0],
+            device_id=across, device_id_type=MESH,
+        ).wait_send)
+    assert len(slots) == recv.shape[0] and len(sent_slots) == send.shape[0]
 
 
 def store(dq_ref, dkv_ref, dq_hbm, dk_hbm, dv_hbm, sem):
@@ -578,7 +578,6 @@
     codes = block_codes.T
     pr = block // ni
     total = STEPS + 1
-    sems = 26
     vmem, hbm = pl.BlockSpec(memory_space=pltpu.VMEM), pl.BlockSpec(memory_space=pltpu.HBM)
     tile = (block, dim)
     grad_q, grad_kv = pl.pallas_call(
@@ -622,8 +621,9 @@
             pltpu.VMEM((2,) + tile, f32),
             pltpu.VMEM((2,) + tile, f32),
             pltpu.VMEM((2, 2) + tile, f32),
-            pltpu.SemaphoreType.DMA((sems,)),
-            pltpu.SemaphoreType.DMA((sems,)),
+            pltpu.VMEM((2 * block + (4 * ni - 3) * pr, dim), f32),
+            pltpu.SemaphoreType.DMA((14,)),
+            pltpu.SemaphoreType.DMA((21,)),
             pltpu.SemaphoreType.REGULAR((2,)),
         ],
         compiler_params=pltpu.CompilerParams(

time: 29.8 us -> 29.6 us (level)
  no operation moved by 1% of the time
where the time goes in v4:
time: 29.6 us; the launch traced here: 29.4 us
  Pallas kernels  27.5 us (93%)
  between operations  1.93 us (7%)
    pallas_call x1, Pallas kernels, shards(): pl.pallas_call(functools.partial(kernel, (ni, no, heads_dev)), out_shape=...  26.8 us
    pallas_call x1, Pallas kernels, shards(): pl.pallas_call(store, out_shape=(jax.ShapeDtypeStruct((rows, dim), f32),...  0.74 us

profile of v4, /device:TPU:0, one launch (start us, length us, event | category | flops | bytes accessed | tf_op | source)
XLA Modules:
  0.0 29.4 jit_solution(2860360732846246743)
XLA Ops:
  1.9 26.8 %shard_map.94 = (f32[512,128]{1,0:T(8,128)S(1)}, f32[128,128]{1,0:T(8,128)S(1)}) custom-call(s32[1]{0:T(128)S(6)} %copy.10.sink_hbm, s32[1]{0:T(128)S(6)} %copy.11.window_hbm, s32[5,16]{1,0:T(8,128)} %bitcast.12, f32[512,128]{1,0:T(8,128)} %bitcast.8, f32[64,128]{1,0:T(8,128)} %bitcast.10, f32[64,128]{1,0:T(8,128)} %bitcast.11, f32[512,128]{1,0:T(8,128)} %bitcast.9), custom_call_target="tpu_custom_call" | custom-call | tf_op jit(solution)/shard_map/pallas_call | solution.py:583
  28.7 0.7 %shard_map.95 = (f32[512,128]{1,0:T(8,128)}, f32[64,128]{1,0:T(8,128)}, f32[64,128]{1,0:T(8,128)}) custom-call(f32[512,128]{1,0:T(8,128)S(1)} %get-tuple-element.8.dq_ref, f32[128,128]{1,0:T(8,128)S(1)} %get-tuple-element.9.dkv_ref), custom_call_target="tpu_custom_call" | custom-call | tf_op jit(solution)/shard_map/pallas_call | solution.py:636

commit v5 on v4

--- a/solution.py
+++ b/solution.py
@@ -426,7 +426,7 @@
         c = copy(f"gz{o}", gout.at[o], gin.at[o], seq(-o))
         when(down(o) & (~at_root(o)), c.start)
 
-    @pl.when(outer == 2)
+    @pl.when(((outer == 2) & (2 * inner < ni)))
     def _():
         give_near(2)
 
@@ -454,7 +454,7 @@
         start("g3", g3out.at[p], g3in.at[p], device, down(3) & end if p else down(3))
     start("g3", g3out.at[1], g3in.at[1], seq(-3), down(3) & jnp.logical_not(end))
 
-    @pl.when(outer != 2)
+    @pl.when(jnp.logical_not(((outer == 2) & (2 * inner < ni))))
     def _():
         give_near(2)
     give_near(1)
@@ -471,7 +471,7 @@
     xout[0] = give
 
     where = pl.ds(pl.multiple_of(inner * pr, pr), pr)
-    @pl.when(outer == 2)
+    @pl.when(((outer == 2) & (2 * inner < ni)))
     def _():
         pass_on(2)
     arrived("b1", sin.at[1:2 * ni])
@@ -485,7 +485,7 @@
                 mine_here = (inner == i) & (outer == z)
                 start("b2", s2, s2in.at[i * no + z], (head, 0, 0), mine_here)
 
-    @pl.when(outer != 2)
+    @pl.when(jnp.logical_not(((outer == 2) & (2 * inner < ni))))
     def _():
         pass_on(2)
     pass_on(1)

time: 29.6 us -> 29.5 us (level)
  no operation moved by 1% of the time
where the time goes in v5:
time: 29.5 us; the launch traced here: 29.3 us
  Pallas kernels  27.4 us (93%)
  between operations  1.93 us (7%)
    pallas_call x1, Pallas kernels, shards(): pl.pallas_call(functools.partial(kernel, (ni, no, heads_dev)), out_shape=...  26.6 us
    pallas_call x1, Pallas kernels, shards(): pl.pallas_call(store, out_shape=(jax.ShapeDtypeStruct((rows, dim), f32),...  0.74 us

profile of v5, /device:TPU:0, one launch (start us, length us, event | category | flops | bytes accessed | tf_op | source)
XLA Modules:
  0.0 29.3 jit_solution(14474433160988646585)
XLA Ops:
  1.9 26.6 %shard_map.94 = (f32[512,128]{1,0:T(8,128)S(1)}, f32[128,128]{1,0:T(8,128)S(1)}) custom-call(s32[1]{0:T(128)S(6)} %copy.10.sink_hbm, s32[1]{0:T(128)S(6)} %copy.11.window_hbm, s32[5,16]{1,0:T(8,128)} %bitcast.12, f32[512,128]{1,0:T(8,128)} %bitcast.8, f32[64,128]{1,0:T(8,128)} %bitcast.10, f32[64,128]{1,0:T(8,128)} %bitcast.11, f32[512,128]{1,0:T(8,128)} %bitcast.9), custom_call_target="tpu_custom_call" | custom-call | tf_op jit(solution)/shard_map/pallas_call | solution.py:583
  28.6 0.7 %shard_map.95 = (f32[512,128]{1,0:T(8,128)}, f32[64,128]{1,0:T(8,128)}, f32[64,128]{1,0:T(8,128)}) custom-call(f32[512,128]{1,0:T(8,128)S(1)} %get-tuple-element.8.dq_ref, f32[128,128]{1,0:T(8,128)S(1)} %get-tuple-element.9.dkv_ref), custom_call_target="tpu_custom_call" | custom-call | tf_op jit(solution)/shard_map/pallas_call | solution.py:636

commit v6 on v5

--- a/solution.py
+++ b/solution.py
@@ -369,8 +369,16 @@
     def _():
         third()
         last(1)
-        last(2)
-        sinks()
+
+        @pl.when(bridged & (outer == 1))
+        def _():
+            sinks()
+            last(2)
+
+        @pl.when(jnp.logical_not(bridged & (outer == 1)))
+        def _():
+            last(2)
+            sinks()
 
     @pl.when(end)
     def _():

time: 29.5 us -> 29.5 us (level)
  no operation moved by 1% of the time
where the time goes in v6:
time: 29.5 us; the launch traced here: 29.3 us
  Pallas kernels  27.4 us (93%)
  between operations  1.93 us (7%)
    pallas_call x1, Pallas kernels, shards(): pl.pallas_call(functools.partial(kernel, (ni, no, heads_dev)), out_shape=...  26.7 us
    pallas_call x1, Pallas kernels, shards(): pl.pallas_call(store, out_shape=(jax.ShapeDtypeStruct((rows, dim), f32),...  0.74 us

profile of v6, /device:TPU:0, one launch (start us, length us, event | category | flops | bytes accessed | tf_op | source)
XLA Modules:
  0.0 29.3 jit_solution(9055437456271982738)
XLA Ops:
  1.9 26.7 %shard_map.94 = (f32[512,128]{1,0:T(8,128)S(1)}, f32[128,128]{1,0:T(8,128)S(1)}) custom-call(s32[1]{0:T(128)S(6)} %copy.10.sink_hbm, s32[1]{0:T(128)S(6)} %copy.11.window_hbm, s32[5,16]{1,0:T(8,128)} %bitcast.12, f32[512,128]{1,0:T(8,128)} %bitcast.8, f32[64,128]{1,0:T(8,128)} %bitcast.10, f32[64,128]{1,0:T(8,128)} %bitcast.11, f32[512,128]{1,0:T(8,128)} %bitcast.9), custom_call_target="tpu_custom_call" | custom-call | tf_op jit(solution)/shard_map/pallas_call | solution.py:591
  28.6 0.7 %shard_map.95 = (f32[512,128]{1,0:T(8,128)}, f32[64,128]{1,0:T(8,128)}, f32[64,128]{1,0:T(8,128)}) custom-call(f32[512,128]{1,0:T(8,128)S(1)} %get-tuple-element.8.dq_ref, f32[128,128]{1,0:T(8,128)S(1)} %get-tuple-element.9.dkv_ref), custom_call_target="tpu_custom_call" | custom-call | tf_op jit(solution)/shard_map/pallas_call | solution.py:644
